TPU v7x, 8 devices: a whole 2x2x1 slice. The times are simulated.
8 devices in a mesh: data: 2 (over z, y), time: 4 (over x, core).
Axes of the slice: x: 2, y: 2, z: 1, core: 2. Of those that a mesh axis runs over, the one named last changes fastest.
Arguments:
- x_init: float32 [32, 256, 768], P('data'), parts along dimension 0
- w_in: bfloat16 [768, 3072], replicated
- w_out: bfloat16 [3072, 768], replicated
- mod_gamma: bfloat16 [16, 3072], P('time')
- mod_beta: bfloat16 [16, 3072], P('time')
- step_size: float32 [16], P('time')
Outputs:
- output: float32 [32, 256, 768], P('data'), parts along dimension 0
There are 2 independent parts. A program takes and returns all parts, laid end to end along the dimension named above; an argument that names none is the same for every part.
All inputs are finite; a program needn't handle non-finite values.
Results may differ from a plain program's by a relative error of at most 0.0018853.
Values are sent between devices in bfloat16 or wider.
A program may use at most 1 GiB of HBM per device.

v0:
```python
import jax
import jax.numpy as jnp
from jax import lax
from jax.sharding import PartitionSpec as P

SWEEPS = 4


def solution(mesh):
    groups = mesh.shape["time"]
    distances = [2 ** level for level in range(12) if 2 ** level < groups]

    def prefix_of(own_total):
        prefix = jnp.zeros_like(own_total)
        inclusive = own_total
        for distance in distances:
            send_pairs = [(source, source + distance) for source in range(groups - distance)]
            received = lax.ppermute(inclusive, "time", send_pairs)
            inclusive = inclusive + received
            prefix = prefix + received
        return prefix

    def local_run(x_init, w_in, w_out, mod_gamma, mod_beta, step_size):
        mod_scale = (1.0 + mod_gamma.astype(jnp.float32))[:, None, None, :]
        mod_shift = mod_beta.astype(jnp.float32)[:, None, None, :]
        h_steps = step_size[:, None, None, None]
        pre_act = jnp.einsum("bnc,cd->bnd", x_init.astype(jnp.bfloat16), w_in, preferred_element_type=jnp.float32)[None]
        result = x_init
        for sweep_idx in range(SWEEPS):
            hidden_act = jax.nn.gelu(pre_act * mod_scale + mod_shift, approximate=True).astype(jnp.bfloat16)
            drifts = jnp.einsum("kbnd,dc->kbnc", hidden_act, w_out, preferred_element_type=jnp.float32) * h_steps
            if sweep_idx < SWEEPS - 1:
                running = jnp.cumsum(drifts, axis=0)
                latents = x_init + prefix_of(running[-1]) + (running - drifts)
                pre_act = jnp.einsum("kbnc,cd->kbnd", latents.astype(jnp.bfloat16), w_in, preferred_element_type=jnp.float32)
            else:
                result = x_init + lax.psum(jnp.sum(drifts, axis=0), "time")
        return result

    return jax.shard_map(local_run, mesh=mesh, in_specs=(P("data", None, None), P(None, None), P(None, None), P("time", None), P("time", None), P("time")), out_specs=P("data", None, None), check_vma=False)
```

profile of v0, /device:TPU:0, one launch (start us, length us, event | category | flops | bytes accessed | tf_op | source)
XLA Modules:
  0.0 2521.6 jit_solution(3828163664904231566)
XLA Ops:
  8.1 31.2 %fusion.49 = f32[16,256,3072]{2,1,0:T(8,128)} fusion(f32[16,256,768]{2,1,0:T(8,128)} %param.6, bf16[768,3072]{1,0:T(8,128)(2,1)} %param.7), kind=kOutput, calls=%fused_computation.62 | convolution fusion | flops 19330498560 | bytes 67633152 | tf_op jit(solution)/shard_map/bnc,cd->bnd/dot_general | solution.py:27
  39.3 140.1 %fusion.32 = f32[4,16,256,768]{3,2,1,0:T(8,128)} fusion(f32[4,3072]{1,0:T(4,128)S(1)} %convert_element_type.32, f32[4,3072]{1,0:T(4,128)S(1)} %convert_add_fusion, f32[16,256,3072]{2,1,0:T(8,128)} %fusion.49, bf16[3072,768]{1,0:T(8,128)(2,1)} %param.8), kind=kOutput, calls=%fused_computation.36 | convolution fusion | flops 77863059456 | bytes 105480192 | tf_op jit(solution)/shard_map/kbnd,dc->kbnc/dot_general | solution.py:31
  179.4 33.2 %fusion.38 = f32[4,16,256,768]{3,2,1,0:T(8,128)} fusion(f32[4,16,256,768]{3,2,1,0:T(8,128)} %fusion.32, f32[4]{0:T(128)S(1)} %copy-done.6), kind=kOutput, calls=%fused_computation.45 | output fusion | flops 50331648 | bytes 100663312 | tf_op jit(solution)/shard_map/jit(cumsum)/reduce_window_sum | solution.py:33
  227.0 18.0 collective-permute-done
  255.5 128.1 %collective-permute-start.1 = (f32[16,256,768]{2,1,0:T(8,128)}, f32[16,256,768]{2,1,0:T(8,128)}, u32[]{:S(2)}, u32[]{:S(2)}) collective-permute-start(f32[16,256,768]{2,1,0:T(8,128)} %fusion.83), channel_id=1, source_target_pairs={{0,2},{1,3},{4,6},{5,7}} | collective-permute-start | bytes 37748744 | tf_op jit(solution)/shard_map/ppermute | solution.py:18
  383.6 262.5 %collective-permute-done.1 = f32[16,256,768]{2,1,0:T(8,128)} collective-permute-done((f32[16,256,768]{2,1,0:T(8,128)}, f32[16,256,768]{2,1,0:T(8,128)}, u32[]{:S(2)}, u32[]{:S(2)}) %collective-permute-start.1) | collective-permute-done | bytes 12582944 | tf_op jit(solution)/shard_map/ppermute | solution.py:18
  646.1 14.3 add_add_fusion.2
  660.4 131.6 %fusion.15.clone.2 = bf16[4,16,256,3072]{3,2,1,0:T(8,128)(2,1)} fusion(f32[4,3072]{1,0:T(4,128)S(1)} %convert_element_type.32, f32[4,3072]{1,0:T(4,128)S(1)} %convert_add_fusion, f32[4,16,256,768]{3,2,1,0:T(8,128)} %fusion.38, f32[4,16,256,768]{3,2,1,0:T(8,128)} %fusion.32, f32[16,256,768]{2,1,0:T(8,128)} %add_add_fusion.2, ...), kind=kOutput, calls=%fused_computation.19.clone.clone.clone | convolution fusion | flops 77913391104 | bytes 218726416 | tf_op jit(solution)/shard_map/kbnc,cd->kbnd/dot_general | solution.py:35
  792.0 86.5 %fusion.60 = f32[4,16,256,768]{3,2,1,0:T(8,128)} fusion(bf16[3072,768]{1,0:T(8,128)(2,1)} %param.8, bf16[4,16,256,3072]{3,2,1,0:T(8,128)(2,1)} %fusion.15.clone.2), kind=kOutput, calls=%fused_computation.68 | convolution fusion | flops 77309411328 | bytes 155713536 | tf_op jit(solution)/shard_map/kbnd,dc->kbnc/dot_general | solution.py:31
  878.5 33.4 %fusion.36 = f32[4,16,256,768]{3,2,1,0:T(8,128)} fusion(f32[4,16,256,768]{3,2,1,0:T(8,128)} %fusion.60, f32[4]{0:T(128)S(1)} %copy-done.7), kind=kOutput, calls=%fused_computation.43 | output fusion | flops 50331648 | bytes 100663312 | tf_op jit(solution)/shard_map/jit(cumsum)/reduce_window_sum | solution.py:33
  924.7 18.0 collective-permute-done.2
  953.3 128.6 %collective-permute-start.3 = (f32[16,256,768]{2,1,0:T(8,128)}, f32[16,256,768]{2,1,0:T(8,128)}, u32[]{:S(2)}, u32[]{:S(2)}) collective-permute-start(f32[16,256,768]{2,1,0:T(8,128)} %fusion.84), channel_id=1, source_target_pairs={{0,2},{1,3},{4,6},{5,7}} | collective-permute-start | bytes 37748744 | tf_op jit(solution)/shard_map/ppermute | solution.py:18
  1081.8 262.5 %collective-permute-done.3 = f32[16,256,768]{2,1,0:T(8,128)} collective-permute-done((f32[16,256,768]{2,1,0:T(8,128)}, f32[16,256,768]{2,1,0:T(8,128)}, u32[]{:S(2)}, u32[]{:S(2)}) %collective-permute-start.3) | collective-permute-done | bytes 12582944 | tf_op jit(solution)/shard_map/ppermute | solution.py:18
  1344.3 14.3 add_add_fusion.1
  1358.6 132.0 %fusion.23.clone.4 = bf16[4,16,256,3072]{3,2,1,0:T(8,128)(2,1)} fusion(f32[4,3072]{1,0:T(4,128)S(1)} %copy-done.4, f32[4,3072]{1,0:T(4,128)S(1)} %copy-done.1, f32[4,16,256,768]{3,2,1,0:T(8,128)} %fusion.36, f32[4,16,256,768]{3,2,1,0:T(8,128)} %fusion.60, f32[16,256,768]{2,1,0:T(8,128)} %add_add_fusion.1, f32[4]{0:T(128)S(1)} %copy-done.7, ...), kind=kOutput, calls=%fused_computation.27.clone.clone.clone.1 | convolution fusion | flops 77913391104 | bytes 218726416 | tf_op jit(solution)/shard_map/kbnc,cd->kbnd/dot_general | solution.py:35
  1490.6 86.5 %fusion.57 = f32[4,16,256,768]{3,2,1,0:T(8,128)} fusion(bf16[3072,768]{1,0:T(8,128)(2,1)} %param.8, bf16[4,16,256,3072]{3,2,1,0:T(8,128)(2,1)} %fusion.23.clone.4), kind=kOutput, calls=%fused_computation.67 | convolution fusion | flops 77309411328 | bytes 155713536 | tf_op jit(solution)/shard_map/kbnd,dc->kbnc/dot_general | solution.py:31
  1577.1 33.6 %fusion.34 = f32[4,16,256,768]{3,2,1,0:T(8,128)} fusion(f32[4,16,256,768]{3,2,1,0:T(8,128)} %fusion.57, f32[4]{0:T(128)S(1)} %copy-done.8), kind=kOutput, calls=%fused_computation.41 | output fusion | flops 50331648 | bytes 100663312 | tf_op jit(solution)/shard_map/jit(cumsum)/reduce_window_sum | solution.py:33
  1623.4 18.0 collective-permute-done.4
  1651.9 128.6 %collective-permute-start.5 = (f32[16,256,768]{2,1,0:T(8,128)}, f32[16,256,768]{2,1,0:T(8,128)}, u32[]{:S(2)}, u32[]{:S(2)}) collective-permute-start(f32[16,256,768]{2,1,0:T(8,128)} %fusion.85), channel_id=1, source_target_pairs={{0,2},{1,3},{4,6},{5,7}} | collective-permute-start | bytes 37748744 | tf_op jit(solution)/shard_map/ppermute | solution.py:18
  1780.5 262.5 %collective-permute-done.5 = f32[16,256,768]{2,1,0:T(8,128)} collective-permute-done((f32[16,256,768]{2,1,0:T(8,128)}, f32[16,256,768]{2,1,0:T(8,128)}, u32[]{:S(2)}, u32[]{:S(2)}) %collective-permute-start.5) | collective-permute-done | bytes 12582944 | tf_op jit(solution)/shard_map/ppermute | solution.py:18
  2043.0 14.3 add_add_fusion
  2057.3 132.0 %fusion.31.clone.4 = bf16[4,16,256,3072]{3,2,1,0:T(8,128)(2,1)} fusion(f32[4,3072]{1,0:T(4,128)S(1)} %copy-done.5, f32[4,3072]{1,0:T(4,128)S(1)} %copy-done.2, f32[4,16,256,768]{3,2,1,0:T(8,128)} %fusion.34, f32[4,16,256,768]{3,2,1,0:T(8,128)} %fusion.57, f32[16,256,768]{2,1,0:T(8,128)} %add_add_fusion, f32[4]{0:T(128)S(1)} %copy-done.8, ...), kind=kOutput, calls=%fused_computation.35.clone.clone.clone.1 | convolution fusion | flops 77913391104 | bytes 218726416 | tf_op jit(solution)/shard_map/kbnc,cd->kbnd/dot_general | solution.py:35
  2189.3 94.2 %multiply_reduce_fusion = f32[16,256,768]{2,1,0:T(8,128)} fusion(f32[4]{0:T(128)S(1)} %copy-done.8, bf16[3072,768]{1,0:T(8,128)(2,1)} %param.8, bf16[4,16,256,3072]{3,2,1,0:T(8,128)(2,1)} %fusion.31.clone.4), kind=kOutput, calls=%fused_computation.37 | convolution fusion | flops 77331431424 | bytes 117964816 | tf_op jit(solution)/shard_map/kbnd,dc->kbnc/dot_general | solution.py:31
  2283.5 217.0 %all-reduce.2.cloned.1.call-done = f32[16,256,768]{2,1,0:T(8,128)} async-done(((f32[16,256,768]{2,1,0:T(8,128)}), f32[16,256,768]{2,1,0:T(8,128)}) %all-reduce.2.cloned.1.call-update) | async-done | bytes 12582928 | tf_op jit(solution)/shard_map/psum | solution.py:37
  (37 shorter events, 87.3 us)
Async XLA Ops:
  6.5 2493.9 %all-reduce.2.cloned.1.call-start = ((), (), s32[]{:S(2)}) async-start(), calls=%async_computation | async-start | bytes 25165824 | tf_op jit(solution)/shard_map/psum | solution.py:37
  7.3 653.1 %copy-start = (f32[4,3072]{1,0:T(4,128)}, f32[4,3072]{1,0:T(4,128)S(1)}, u32[]{:S(2)}) copy-start(f32[4,3072]{1,0:T(4,128)S(1)} %convert_add_fusion) | copy-start | bytes 147460
  8.1 652.3 %copy-start.3 = (f32[4,3072]{1,0:T(4,128)}, f32[4,3072]{1,0:T(4,128)S(1)}, u32[]{:S(2)}) copy-start(f32[4,3072]{1,0:T(4,128)S(1)} %convert_element_type.32) | copy-start | bytes 147460
  39.3 140.1 %copy-start.6 = (f32[4]{0:T(128)S(1)}, f32[4]{0:T(128)}, u32[]{:S(2)}) copy-start(f32[4]{0:T(128)} %param.11) | copy-start | bytes 52
  223.2 437.2 %slice-start = ((s8[4718592]{0:T(1024)(128)(4,1)}), s8[4194304]{0:T(1024)(128)(4,1)S(1)}, s32[]{:S(2)}) async-start(s8[4718592]{0:T(1024)(128)(4,1)} %bitcast.54), calls=%async_computation.1 | async-start | bytes 8388608
  223.2 21.8 collective-permute-start
  255.5 404.8 %slice-start.1 = ((s8[4718592]{0:T(1024)(128)(4,1)}), s8[524288]{0:T(1024)(128)(4,1)S(1)}, s32[]{:S(2)}) async-start(s8[4718592]{0:T(1024)(128)(4,1)} %bitcast.54), calls=%async_computation.2 | async-start | bytes 1048576
  255.5 390.5 %collective-permute-start.1 = (f32[16,256,768]{2,1,0:T(8,128)}, f32[16,256,768]{2,1,0:T(8,128)}, u32[]{:S(2)}, u32[]{:S(2)}) collective-permute-start(f32[16,256,768]{2,1,0:T(8,128)} %fusion.83), channel_id=1, source_target_pairs={{0,2},{1,3},{4,6},{5,7}} | collective-permute-start | bytes 37748744 | tf_op jit(solution)/shard_map/ppermute | solution.py:18
  792.0 86.5 %copy-start.7 = (f32[4]{0:T(128)S(1)}, f32[4]{0:T(128)}, u32[]{:S(2)}) copy-start(f32[4]{0:T(128)} %param.11) | copy-start | bytes 52
  922.5 436.1 %copy-start.1 = (f32[4,3072]{1,0:T(4,128)S(1)}, f32[4,3072]{1,0:T(4,128)}, u32[]{:S(2)}) copy-start(f32[4,3072]{1,0:T(4,128)} %copy-done) | copy-start | bytes 147460
  922.5 436.1 %copy-start.4 = (f32[4,3072]{1,0:T(4,128)S(1)}, f32[4,3072]{1,0:T(4,128)}, u32[]{:S(2)}) copy-start(f32[4,3072]{1,0:T(4,128)} %copy-done.3) | copy-start | bytes 147460
  922.5 20.2 collective-permute-start.2
  953.3 391.1 %collective-permute-start.3 = (f32[16,256,768]{2,1,0:T(8,128)}, f32[16,256,768]{2,1,0:T(8,128)}, u32[]{:S(2)}, u32[]{:S(2)}) collective-permute-start(f32[16,256,768]{2,1,0:T(8,128)} %fusion.84), channel_id=1, source_target_pairs={{0,2},{1,3},{4,6},{5,7}} | collective-permute-start | bytes 37748744 | tf_op jit(solution)/shard_map/ppermute | solution.py:18
  1490.6 86.5 %copy-start.8 = (f32[4]{0:T(128)S(1)}, f32[4]{0:T(128)}, u32[]{:S(2)}) copy-start(f32[4]{0:T(128)} %param.11) | copy-start | bytes 52
  1610.7 446.5 %copy-start.2 = (f32[4,3072]{1,0:T(4,128)S(1)}, f32[4,3072]{1,0:T(4,128)}, u32[]{:S(2)}) copy-start(f32[4,3072]{1,0:T(4,128)} %copy-done) | copy-start | bytes 147460
  1610.7 446.5 %copy-start.5 = (f32[4,3072]{1,0:T(4,128)S(1)}, f32[4,3072]{1,0:T(4,128)}, u32[]{:S(2)}) copy-start(f32[4,3072]{1,0:T(4,128)} %copy-done.3) | copy-start | bytes 147460
  1621.3 20.1 collective-permute-start.4
  1651.9 391.1 %collective-permute-start.5 = (f32[16,256,768]{2,1,0:T(8,128)}, f32[16,256,768]{2,1,0:T(8,128)}, u32[]{:S(2)}, u32[]{:S(2)}) collective-permute-start(f32[16,256,768]{2,1,0:T(8,128)} %fusion.85), channel_id=1, source_target_pairs={{0,2},{1,3},{4,6},{5,7}} | collective-permute-start | bytes 37748744 | tf_op jit(solution)/shard_map/ppermute | solution.py:18
Sparse Core Ops, SparseCore 0:
  2283.6 216.8 all-reduce.1
where the time goes:
time: 2530 us; the launch traced here: 2520 us
  waiting for transfers between devices  1060 us (42%)
  matrix products  834 us (33%)
  starting transfers between devices  393 us (16%)
  other arithmetic  190 us (8%)
  local copies, waits for them, and re-layouts  31.8 us (1%)
    ppermute x6, waiting for transfers between devices, prefix_of(): received = lax.ppermute(inclusive, 'time', send_pairs)  841 us
    dot_general x4, matrix products, local_run(): jnp.einsum('kbnd,dc->kbnc', hidden_act, w_out, preferred_element_type=jnp...  407 us
    dot_general x3, matrix products, local_run(): jnp.einsum('kbnc,cd->kbnd', latents.astype(jnp.bfloat16), w_in, preferred...  396 us
    ppermute x6, starting transfers between devices, prefix_of(): received = lax.ppermute(inclusive, 'time', send_pairs)  393 us
    psum x1, waiting for transfers between devices, local_run(): result = x_init + lax.psum(jnp.sum(drifts, axis=0), 'time')  217 us
    another operation x3, other arithmetic, local_run(): running = jnp.cumsum(drifts, axis=0)  100 us
  transfers between devices with their start and end apart: 7, of which 7 were waited for; matrix products, arithmetic and copies ran while one was open for 0% of the time, Pallas kernels for 0%

commit v1 on v0

v1 whole, which is shorter than its diff:
```python
import jax
import jax.numpy as jnp
from jax import lax
from jax.experimental import pallas as pl
from jax.experimental.pallas import tpu as pltpu
from jax.sharding import PartitionSpec as P

R = 256
C = 768
D = 3072
T = 16
NB = D // 256
K2 = 2.0 * 0.7978845608028654
K3 = 8.0 * 0.7978845608028654 * 0.044715

def gelu_mod(a, g, b):
    u = a * g + b
    p = (u * u) * K3 + K2
    t = jnp.tanh(u * p)
    return (u * t + u).astype(jnp.bfloat16)

def kernel(t_ref, x_ref, win_ref, wout_ref, g_ref, b_ref, h_ref, hs_ref, o_ref, a0, lat, latb, hid, s_acc):
    xb = x_ref[...].astype(jnp.bfloat16)
    for n in range(NB):
        a0[:, n * 256:(n + 1) * 256] = jnp.dot(xb, win_ref[:, n * 256:(n + 1) * 256], preferred_element_type=jnp.float32)
    s_acc[...] = jnp.zeros_like(s_acc)

    def step(j, lo, hi, fresh):
        lo1 = max(lo, 1)
        r0, r1 = (lo1 - 1) * R, hi * R
        for n in range(NB):
            cs = slice(n * 256, (n + 1) * 256)
            g = g_ref[pl.ds(j, 1), cs]
            b = b_ref[pl.ds(j, 1), cs]
            if lo == 0:
                hid[0:R, cs] = gelu_mod(a0[:, cs], g, b)
            if hi >= 1:
                a = jnp.dot(latb[r0:r1, :], win_ref[:, cs], preferred_element_type=jnp.float32)
                hv = gelu_mod(a, g, b)
                for s in range(lo1, hi + 1):
                    part = hv[(s - lo1) * R:(s - lo1 + 1) * R]
                    if s <= 2:
                        hid[s * R:(s + 1) * R, cs] = part
                    else:
                        s_acc[:, cs] += part.astype(jnp.float32) * hs_ref[pl.ds(j, 1), cs]
        hi2 = min(hi, 2)
        if lo <= hi2:
            for m in range(3):
                ms = slice(m * 256, (m + 1) * 256)
                d = jnp.dot(hid[lo * R:(hi2 + 1) * R, :], wout_ref[:, ms], preferred_element_type=jnp.float32)
                d = d * h_ref[pl.ds(j, 1), ms]
                for s in reversed(range(lo, hi2 + 1)):
                    rs = slice(s * R, (s + 1) * R)
                    if s == fresh:
                        base = x_ref[:, ms] if s == 0 else lat[(s - 1) * R:s * R, ms]
                    else:
                        base = lat[rs, ms]
                    new = base + d[(s - lo) * R:(s - lo + 1) * R]
                    lat[rs, ms] = new
                    latb[rs, ms] = new.astype(jnp.bfloat16)

    step(0, 0, 0, 0)
    step(1, 0, 1, 1)
    step(2, 0, 2, 2)
    o_ref[...] = lat[2 * R:3 * R, :]
    @pl.loop(3, 13)
    def _(j):
        step(j, 0, 3, -1)
    step(13, 1, 3, -1)
    step(14, 2, 3, -1)
    step(15, 3, 3, -1)
    for n in range(NB):
        cs = slice(n * 256, (n + 1) * 256)
        sv = s_acc[:, cs]
        hi_ = sv.astype(jnp.bfloat16)
        r = sv - hi_.astype(jnp.float32)
        mid = r.astype(jnp.bfloat16)
        hid[0:R, cs] = hi_
        hid[R:2 * R, cs] = mid
        hid[2 * R:3 * R, cs] = (r - mid.astype(jnp.float32)).astype(jnp.bfloat16)
    for m in range(3):
        ms = slice(m * 256, (m + 1) * 256)
        d = jnp.dot(hid[...], wout_ref[:, ms], preferred_element_type=jnp.float32)
        o_ref[:, ms] = o_ref[:, ms] + (d[0:R] + (d[R:2 * R] + d[2 * R:3 * R])) * h_ref[T:T + 1, ms]


def solution(mesh):
    groups = mesh.shape["time"]

    def local_run(x_init, w_in, w_out, mod_gamma, mod_beta, step_size):
        samples, tokens, _ = x_init.shape
        rows = samples * tokens // groups
        me = lax.axis_index("time")
        gamma = lax.all_gather(mod_gamma, "time", tiled=True).astype(jnp.float32)
        beta = lax.all_gather(mod_beta, "time", tiled=True).astype(jnp.float32)
        h = lax.all_gather(step_size, "time", tiled=True)
        top = jnp.max(jnp.abs(h)) * 16.0
        scale = jnp.where(top > 0, h / top, 0.0)
        hb = jnp.concatenate([jnp.broadcast_to(h[:, None], (T, C)), jnp.full((8, C), top)], 0)
        hs = jnp.broadcast_to(scale[:, None], (T, D))
        steps = rows // R
        full = lambda a: pl.BlockSpec(a.shape, lambda i, t: (0,) * a.ndim, pipeline_mode=pl.Buffered(1))
        args = (w_in, w_out, 0.5 + 0.5 * gamma, 0.5 * beta, hb, hs)
        out = pl.pallas_call(
            kernel,
            grid_spec=pltpu.PrefetchScalarGridSpec(
                num_scalar_prefetch=1, grid=(steps,),
                in_specs=[pl.BlockSpec((R, C), lambda i, t: (t[0] * steps + i, 0))] + [full(a) for a in args],
                out_specs=pl.BlockSpec((R, C), lambda i, t: (i, 0)),
                scratch_shapes=[pltpu.VMEM((R, D), jnp.float32), pltpu.VMEM((3 * R, C), jnp.float32),
                                pltpu.VMEM((3 * R, C), jnp.bfloat16), pltpu.VMEM((3 * R, D), jnp.bfloat16),
                                pltpu.VMEM((R, D), jnp.float32)],
            ),
            out_shape=jax.ShapeDtypeStruct((rows, C), jnp.float32),
            compiler_params=pltpu.CompilerParams(vmem_limit_bytes=60 * 2**20),
        )(me.astype(jnp.int32).reshape(1), x_init.reshape(-1, C), *args)
        return lax.all_gather(out, "time", tiled=True).reshape(x_init.shape)

    return jax.shard_map(local_run, mesh=mesh, in_specs=(P("data", None, None), P(None, None), P(None, None), P("time", None), P("time", None), P("time")), out_specs=P("data", None, None), check_vma=False)
```

time: 2530 us -> 668 us (0.26)
  waiting for transfers between devices: 1060 us -> 80.3 us
  matrix products: 834 us -> 0 us
  Pallas kernels: 0 us -> 531 us
  starting transfers between devices: 393 us -> 0.01 us
  other arithmetic: 190 us -> 0.71 us
    ppermute x6 -> x0, waiting for transfers between devices: 841 us -> none  [prefix_of(): received = lax.ppermute(inclusive, 'time', send_pairs)]
    dot_general x8 -> x0, matrix products: 834 us -> none  [the longest x4 407 us: local_run(): jnp.einsum('kbnd,dc->kbnc', hidden_act, w_out, preferred_element_type=jnp...]
    pallas_call x0 -> x1, Pallas kernels: none -> 531 us  [local_run(): pl.pallas_call(kernel, grid_spec=pltpu.PrefetchScalarGridSpec(num_scalar_...]
    ppermute x6 -> x0, starting transfers between devices: 393 us -> none  [prefix_of(): received = lax.ppermute(inclusive, 'time', send_pairs)]
    psum x1 -> x0, waiting for transfers between devices: 217 us -> none  [local_run(): result = x_init + lax.psum(jnp.sum(drifts, axis=0), 'time')]
    another operation x3 -> x0, other arithmetic: 100 us -> none  [local_run(): running = jnp.cumsum(drifts, axis=0)]
    add x8 -> x1, other arithmetic: 89.4 us -> 0.05 us  [local_run(): args = (w_in, w_out, 0.5 + 0.5 * gamma, 0.5 * beta, hb, hs)]
    all_gather x0 -> x1, waiting for transfers between devices: none -> 80.3 us  [local_run(): return lax.all_gather(out, 'time', tiled=True).reshape(x_init.shape)]
  transfers between devices with their start and end apart: 7 -> 1, of which waited for: 7 -> 1; matrix products, arithmetic and copies ran while one was open for 0% -> 0% of each run, Pallas kernels for 0% -> 0%
where the time goes in v1:
time: 668 us; the launch traced here: 666 us
  Pallas kernels  531 us (79%)
  waiting for transfers between devices  80.3 us (12%)
  blocking collectives  24.4 us (4%)
  local copies, waits for them, and re-layouts  15.6 us (2%)
  between operations  14.9 us (2%)
    pallas_call x1, Pallas kernels, local_run(): pl.pallas_call(kernel, grid_spec=pltpu.PrefetchScalarGridSpec(num_scalar_...  531 us
    all_gather x1, waiting for transfers between devices, local_run(): return lax.all_gather(out, 'time', tiled=True).reshape(x_init.shape)  80.3 us
  transfers between devices with their start and end apart: 1, of which 1 were waited for; matrix products, arithmetic and copies ran while one was open for 0% of the time, Pallas kernels for 0%

profile of v1, /device:TPU:0, one launch (start us, length us, event | category | flops | bytes accessed | tf_op | source)
XLA Modules:
  0.0 666.5 jit_solution(10194683059611803818)
XLA Ops:
  6.5 0.0 all-gather.4.cloned.1.call-start
  6.5 1.2 dynamic-slice
  8.4 0.9 dynamic-update-slice
  9.3 8.7 %all-reduce.1 = f32[16]{0:T(128)S(1)} all-reduce(f32[16]{0:T(128)S(1)} %dynamic-update-slice), channel_id=1, replica_groups=mesh['data'=2,'time'=4] {'time'}, use_global_device_ids=true, to_apply=%add.1 | all-reduce | flops 16 | bytes 128
  18.0 0.6 abs_reduce_fusion
  19.3 7.5 %all-gather = bf16[4,4,3072]{2,1,0:T(4,128)(2,1)S(1)} all-gather(bf16[1,4,3072]{2,1,0:T(4,128)(2,1)} %bitcast.8), channel_id=1, replica_groups=mesh['data'=2,'time'=4] {'time'}, dimensions={0}, use_global_device_ids=true | all-gather | bytes 122880 | tf_op jit(solution)/shard_map/all_gather | solution.py:94
  26.8 0.1 multiply_add_fusion
  26.9 0.7 reshape.30.g_ref
  27.6 8.1 %all-gather.1 = bf16[4,4,3072]{2,1,0:T(4,128)(2,1)S(1)} all-gather(bf16[1,4,3072]{2,1,0:T(4,128)(2,1)} %bitcast.9), channel_id=1, replica_groups=mesh['data'=2,'time'=4] {'time'}, dimensions={0}, use_global_device_ids=true | all-gather | bytes 122880 | tf_op jit(solution)/shard_map/all_gather | solution.py:95
  35.8 0.7 reshape.28.b_ref
  36.5 0.7 concatenate.6.h_ref
  37.2 0.7 broadcast_in_dim.7.hs_ref
  38.0 530.5 %shard_map.64 = f32[1024,768]{1,0:T(8,128)} custom-call(s32[1]{0:T(128)} %bitcast.t_ref, f32[4096,768]{1,0:T(8,128)} %bitcast.7, bf16[768,3072]{1,0:T(8,128)(2,1)} %win_ref.1, bf16[3072,768]{1,0:T(8,128)(2,1)} %wout_ref.1, f32[16,3072]{1,0:T(8,128)} %reshape.30.g_ref, f32[16,3072]{1,0:T(8,128)} %reshape.28.b_ref, f32[24,768]{1,0:T(8,128)} %concatenate.6.h_ref, ...), custom_call_target="tpu_custom_call" | custom-call | tf_op jit(solution)/shard_map/pallas_call | solution.py:104
  568.5 0.0 all-gather.4.cloned.1.call-update
  568.5 80.3 %all-gather.4.cloned.1.call-done = f32[4096,768]{1,0:T(8,128)} async-done(((f32[1024,768]{1,0:T(8,128)}), f32[4096,768]{1,0:T(8,128)}) %all-gather.4.cloned.1.call-update) | async-done | bytes 12582928 | tf_op jit(solution)/shard_map/all_gather | solution.py:117
  648.8 10.6 %copy.9 = f32[16,256,768]{2,1,0:T(8,128)} copy(f32[16,256,768]{2,1,0:T(8,128)} %bitcast.6) | data formatting | bytes 25165824
  (4 shorter events, 0.1 us)
Async XLA Ops:
  6.5 642.3 %all-gather.4.cloned.1.call-start = ((), (), s32[]{:S(2)}) async-start(), calls=%async_computation | async-start | bytes 15728640 | tf_op jit(solution)/shard_map/all_gather | solution.py:117
Sparse Core Ops, SparseCore 0:
  568.7 80.1 all-gather.3
